TPU v7x, 32 devices: a whole 2x2x4 slice. The times are simulated.
32 devices in a mesh: seq: 8 (over z, x), tensor: 4 (over y, core).
Axes of the slice: x: 2, y: 2, z: 4, core: 2. Of those that a mesh axis runs over, the one named last changes fastest.
Arguments:
- tokens: bfloat16 [4096, 2048], P('seq', 'tensor'), may hold values from -12 to 12
- attn_gain: float32 [2048], replicated, may hold values from 0.1 to 1.9
- w_query: bfloat16 [2048, 2048], P('seq', 'tensor'), as said below
- w_key: bfloat16 [2048, 512], P('seq', 'tensor'), as said below
- w_value: bfloat16 [2048, 512], P('seq', 'tensor'), may hold values from -0.125 to 0.125
- w_out: bfloat16 [2048, 2048], P('tensor', 'seq'), may hold values from -0.125 to 0.125
- mlp_gain: float32 [2048], replicated, may hold values from 0.1 to 1.9
- w_gate: bfloat16 [2048, 5632], P('seq', 'tensor'), may hold values from -0.125 to 0.125
- w_up: bfloat16 [2048, 5632], P('seq', 'tensor'), may hold values from -0.125 to 0.125
- w_down: bfloat16 [5632, 2048], P('tensor', 'seq'), may hold values from -0.078125 to 0.078125
Outputs:
- layer_out: bfloat16 [4096, 2048], P('seq', 'tensor')
Inputs may be any that keep to these rules, and one draw needn't show every extreme that they name: `w_query`: entries are of order 2048 to the power -1/2. `w_key`: entries are of order 2048 to the power -1/2.
All inputs are finite; a program needn't handle non-finite values.
Results may differ from a plain program's by a relative error of at most 0.013.
Values may be sent and summed in bfloat16 or wider, within the bound.
A program may use at most 128 MiB of HBM per device.

v0:
```python
import jax
import jax.numpy as jnp
from jax import lax
from jax.sharding import PartitionSpec as P

HEAD_DIM = 128
WINDOW = 1024


def passed_along(block, axis, distance):
    devices = range(lax.axis_size(axis))
    route = [(i - distance, i) for i in devices if i - distance in devices]
    return lax.ppermute(block, axis, route)


def scaled_rows(values, gain):
    values = values.astype(jnp.float32)
    mean_square = jnp.mean(values * values, axis=1, keepdims=True)
    return (values * lax.rsqrt(mean_square + 1e-06) * gain).astype(jnp.bfloat16)


def product(left, right):
    return jnp.dot(left, right, preferred_element_type=jnp.float32)


def window_attention(queries, context_keys, context_values, reach, position):
    rows = queries.shape[0]
    local_kv = context_keys.shape[1] // HEAD_DIM
    group = queries.shape[1] // (local_kv * HEAD_DIM)
    block = min(512, rows)
    span = WINDOW + block
    scale = HEAD_DIM ** (-0.5)
    start = reach * rows - WINDOW
    query_block = queries.reshape(block, local_kv, group, HEAD_DIM)
    key_block = context_keys.reshape(span, local_kv, HEAD_DIM)
    value_block = context_values.reshape(span, local_kv, HEAD_DIM)
    scores = (
        jnp.einsum("qkgd,ckd->kgqc", query_block, key_block, preferred_element_type=jnp.float32)
        * scale
    )
    query_pos = lax.broadcasted_iota(jnp.int32, (block, span), 0)
    key_pos = lax.broadcasted_iota(jnp.int32, (block, span), 1)
    distance = query_pos + WINDOW - key_pos
    first_key = (position - reach) * rows + start
    allowed = (distance >= 0) & (distance < WINDOW) & (key_pos + first_key >= 0)
    scores = jnp.where(allowed[None, None], scores, -1e30)
    highest = jnp.max(scores, axis=3, keepdims=True)
    raised = jnp.exp(scores - highest)
    weights = (raised / jnp.sum(raised, axis=3, keepdims=True)).astype(jnp.bfloat16)
    mixed = jnp.einsum("kgqc,ckd->qkgd", weights, value_block, preferred_element_type=jnp.float32)
    outputs = mixed.astype(jnp.bfloat16).reshape(block, local_kv * group * HEAD_DIM)
    return outputs


def per_device(tokens, attn_gain, w_query, w_key, w_value, w_out, mlp_gain, w_gate, w_up, w_down):
    rows = tokens.shape[0]
    whole = lax.all_gather(tokens, "tensor", axis=1, tiled=True)
    normed = scaled_rows(whole, attn_gain)
    query_full = lax.all_gather(w_query, "seq", axis=0, tiled=True)
    key_full, value_full = (
        lax.all_gather(w_key, "seq", axis=0, tiled=True),
        lax.all_gather(w_value, "seq", axis=0, tiled=True),
    )
    queries = product(normed, query_full).astype(jnp.bfloat16)
    keys = product(normed, key_full).astype(jnp.bfloat16)
    values = product(normed, value_full).astype(jnp.bfloat16)
    reach = -(-WINDOW // rows)
    earlier = []
    for step in range(reach):
        earlier.append(passed_along((keys, values), "seq", step + 1))
    context_keys = jnp.concatenate(
        [earlier[reach - 1 - step][0] for step in range(reach)] + [keys], axis=0
    )
    context_values = jnp.concatenate(
        [earlier[reach - 1 - step][1] for step in range(reach)] + [values], axis=0
    )
    position = lax.axis_index("seq")
    attended = window_attention(queries, context_keys, context_values, reach, position)
    out_full = lax.all_gather(w_out, "seq", axis=1, tiled=True)
    head_terms = product(attended, out_full)
    share = tokens.shape[1]
    attn_whole = lax.psum(head_terms.astype(jnp.bfloat16), "tensor").astype(jnp.float32)
    stream_whole = (whole.astype(jnp.float32) + attn_whole).astype(jnp.bfloat16)
    stream_share = lax.dynamic_slice_in_dim(
        stream_whole, lax.axis_index("tensor") * share, share, 1
    )
    stream_normed = scaled_rows(stream_whole, mlp_gain)
    gate_full = lax.all_gather(w_gate, "seq", axis=0, tiled=True)
    up_full = lax.all_gather(w_up, "seq", axis=0, tiled=True)
    gate = product(stream_normed, gate_full)
    upward = product(stream_normed, up_full)
    hidden = (jax.nn.silu(gate) * upward).astype(jnp.bfloat16)
    down_full = lax.all_gather(w_down, "seq", axis=1, tiled=True)
    unit_terms = product(hidden, down_full)
    mlp_share = lax.psum_scatter(
        unit_terms.astype(jnp.bfloat16), "tensor", scatter_dimension=1, tiled=True
    ).astype(jnp.float32)
    return (stream_share.astype(jnp.float32) + mlp_share).astype(jnp.bfloat16)


def solution(mesh):
    in_specs = (
        P("seq", "tensor"),
        P(),
        P("seq", "tensor"),
        P("seq", "tensor"),
        P("seq", "tensor"),
        P("tensor", "seq"),
        P(),
        P("seq", "tensor"),
        P("seq", "tensor"),
        P("tensor", "seq"),
    )
    out_specs = P("seq", "tensor")
    return jax.shard_map(
        per_device, mesh=mesh, in_specs=in_specs, out_specs=out_specs, check_vma=False
    )
```

profile of v0, /device:TPU:0, one launch (start us, length us, event | category | flops | bytes accessed | tf_op | source)
XLA Modules:
  0.0 529.0 jit_solution(15447656682437301794)
XLA Ops:
  6.5 0.0 copy-start.3
  6.5 0.0 all-gather.7.cloned.1.call-start
  6.5 0.7 all-gather.7.cloned.1.call-update
  7.3 0.0 all-gather.9.cloned.1.call-start
  7.3 0.7 all-gather.9.cloned.1.call-update
  8.0 0.0 all-gather.11.cloned.1.call-start
  8.1 0.7 all-gather.11.cloned.1.call-update
  8.7 0.0 all-reduce.2.cloned.1.call-start
  8.8 33.4 %all_gather.26 = bf16[2048,128]{1,0:T(8,128)(2,1)S(1)} all-gather(bf16[256,128]{1,0:T(8,128)(2,1)} %param.13), channel_id=1, replica_groups=mesh['seq'=8,'tensor'=4] {'seq'}, dimensions={0}, use_global_device_ids=true | all-gather | bytes 589824 | tf_op jit(solution)/shard_map/all_gather | solution.py:61
  42.2 35.2 %all_gather.25 = bf16[2048,128]{1,0:T(8,128)(2,1)} all-gather(bf16[256,128]{1,0:T(8,128)(2,1)} %param.14), channel_id=1, replica_groups=mesh['seq'=8,'tensor'=4] {'seq'}, dimensions={0}, use_global_device_ids=true | all-gather | bytes 589824 | tf_op jit(solution)/shard_map/all_gather | solution.py:62
  77.3 1.3 fusion.14
  78.6 0.0 all-gather.7.cloned.1.call-done
  78.6 0.0 copy-start
  78.7 0.0 copy-start.2
  78.7 2.2 fusion.7
  80.9 0.0 copy-done.3
  80.9 2.4 convolution_convert_fusion.3
  83.3 1.3 collective-permute-start.2
  84.6 4.3 collective-permute-start.3
  88.9 0.0 copy-done
  88.9 0.0 copy-done.2
  88.9 0.8 convolution_convert_fusion.4
  89.6 2.7 collective-permute-start
  92.4 2.7 collective-permute-start.1
  95.1 0.0 all-gather.9.cloned.1.call-done
  95.1 3.0 convolution_convert_fusion.2
  98.1 0.0 collective-permute-done.2
  98.1 0.0 collective-permute-done.3
  98.1 3.3 fusion.1
  101.4 2.8 fusion
  104.2 0.0 collective-permute-done
  104.2 0.0 collective-permute-done.1
  104.2 4.8 fusion.16
  109.0 33.7 %all-gather.11.cloned.1.call-done = bf16[512,2048]{1,0:T(8,128)(2,1)} async-done(((bf16[512,256]{1,0:T(8,128)(2,1)}), bf16[512,2048]{1,0:T(8,128)(2,1)}) %all-gather.11.cloned.1.call-update) | async-done | bytes 2097168 | tf_op jit(solution)/shard_map/all_gather | solution.py:79
  142.7 4.4 convolution_convert_fusion
  147.1 0.0 all-reduce.2.cloned.1.call-update
  147.1 0.0 copy-start.4
  147.1 0.0 all-gather.13.cloned.1.call-start
  147.2 0.5 all-gather.13.cloned.1.call-update
  147.7 0.0 all-gather.15.cloned.1.call-start
  147.8 0.5 all-gather.15.cloned.1.call-update
  148.3 0.0 all-gather.17.cloned.1.call-start
  148.4 0.7 all-gather.17.cloned.1.call-update
  149.1 0.3 reduce-scatter.2.cloned.1.call-start
  149.3 47.5 %all-reduce.2.cloned.1.call-done = bf16[512,2048]{1,0:T(8,128)(2,1)} async-done(((bf16[512,2048]{1,0:T(8,128)(2,1)}), bf16[512,2048]{1,0:T(8,128)(2,1)}) %all-reduce.2.cloned.1.call-update) | async-done | bytes 2097168 | tf_op jit(solution)/shard_map/psum | solution.py:82
  196.9 3.9 fusion.4
  200.8 90.5 %all-gather.13.cloned.1.call-done = bf16[2048,1408]{1,0:T(8,128)(2,1)} async-done(((bf16[256,1408]{1,0:T(8,128)(2,1)}), bf16[2048,1408]{1,0:T(8,128)(2,1)}) %all-gather.13.cloned.1.call-update) | async-done | bytes 5767184 | tf_op jit(solution)/shard_map/all_gather | solution.py:88
  291.3 0.0 copy-done.4
  291.3 0.0 copy-start.1
  291.3 8.4 %fusion.21 = f32[512,1408]{1,0:T(8,128)} fusion(bf16[2048,1408]{1,0:T(8,128)(2,1)} %all-gather.13.cloned.1.call-done, bf16[512,2048]{1,0:T(8,128)(2,1)} %get-tuple-element.6, f32[2048]{0:T(1024)S(1)} %copy-done.4, f32[512]{0:T(512)S(1)} %add_rsqrt_fusion), kind=kOutput, calls=%fused_computation.33 | convolution fusion | flops 2956984320 | bytes 10758144 | tf_op jit(solution)/shard_map/dot_general | solution.py:23
  299.7 84.1 %all-gather.15.cloned.1.call-done = bf16[2048,1408]{1,0:T(8,128)(2,1)} async-done(((bf16[256,1408]{1,0:T(8,128)(2,1)}), bf16[2048,1408]{1,0:T(8,128)(2,1)}) %all-gather.15.cloned.1.call-update) | async-done | bytes 5767184 | tf_op jit(solution)/shard_map/all_gather | solution.py:89
  383.9 93.4 %all-gather.17.cloned.1.call-done = bf16[1408,2048]{1,0:T(8,128)(2,1)} async-done(((bf16[1408,256]{1,0:T(8,128)(2,1)}), bf16[1408,2048]{1,0:T(8,128)(2,1)}) %all-gather.17.cloned.1.call-update) | async-done | bytes 5767184 | tf_op jit(solution)/shard_map/all_gather | solution.py:93
  477.2 0.0 copy-done.1
  477.2 13.4 %convolution_convert_fusion.1 = bf16[512,2048]{1,0:T(8,128)(2,1)} fusion(bf16[1408,2048]{1,0:T(8,128)(2,1)} %all-gather.17.cloned.1.call-done, bf16[2048,1408]{1,0:T(8,128)(2,1)} %all-gather.15.cloned.1.call-done, f32[512,1408]{1,0:T(8,128)} %fusion.21, bf16[512,2048]{1,0:T(8,128)(2,1)S(1)} %copy-done.1, f32[2048]{0:T(1024)S(1)} %copy-done.4, ...), kind=kOutput, calls=%fused_computation.27 | convolution fusion | flops 5915148288 | bytes 18622464 | tf_op jit(solution)/shard_map/dot_general | solution.py:23
  490.7 0.0 reduce-scatter.2.cloned.1.call-update
  490.7 29.5 %reduce-scatter.2.cloned.1.call-done = bf16[512,512]{1,0:T(8,128)(2,1)} async-done(((bf16[512,2048]{1,0:T(8,128)(2,1)}), bf16[512,512]{1,0:T(8,128)(2,1)}) %reduce-scatter.2.cloned.1.call-update) | async-done | bytes 524304 | tf_op jit(solution)/shard_map/reduce_scatter | solution.py:95
  520.2 2.0 add_convert_fusion
  (4 shorter events, 0.0 us)
Async XLA Ops:
  6.5 74.4 %copy-start.3 = (f32[2048]{0:T(1024)S(1)}, f32[2048]{0:T(1024)}, u32[]{:S(2)}) copy-start(f32[2048]{0:T(1024)} %param.11) | copy-start | bytes 24580
  6.5 72.1 %all-gather.7.cloned.1.call-start = ((), (), s32[]{:S(2)}) async-start(), calls=%async_computation.1 | async-start | bytes 2621440 | tf_op jit(solution)/shard_map/all_gather | solution.py:57
  7.3 87.8 %all-gather.9.cloned.1.call-start = ((), (), s32[]{:S(2)}) async-start(), calls=%async_computation.2 | async-start | bytes 2359296 | tf_op jit(solution)/shard_map/all_gather | solution.py:59
  8.0 134.7 %all-gather.11.cloned.1.call-start = ((), (), s32[]{:S(2)}) async-start(), calls=%async_computation.3 | async-start | bytes 2359296 | tf_op jit(solution)/shard_map/all_gather | solution.py:79
  8.7 188.1 %all-reduce.2.cloned.1.call-start = ((), (), s32[]{:S(2)}) async-start(), calls=%async_computation.4 | async-start | bytes 4194304 | tf_op jit(solution)/shard_map/psum | solution.py:82
  78.6 10.2 %copy-start = (bf16[512,2048]{1,0:T(8,128)(2,1)S(1)}, bf16[512,2048]{1,0:T(8,128)(2,1)}, u32[]{:S(2)}) copy-start(bf16[512,2048]{1,0:T(8,128)(2,1)} %all-gather.7.cloned.1.call-done) | copy-start | bytes 6291460
  78.7 10.2 %copy-start.2 = (bf16[2048,128]{1,0:T(8,128)(2,1)S(1)}, bf16[2048,128]{1,0:T(8,128)(2,1)}, u32[]{:S(2)}) copy-start(bf16[2048,128]{1,0:T(8,128)(2,1)} %all_gather.25) | copy-start | bytes 1572868
  83.3 14.8 %collective-permute-start.2 = (bf16[512,128]{1,0:T(8,128)(2,1)S(1)}, bf16[512,128]{1,0:T(8,128)(2,1)S(1)}, u32[]{:S(2)}, u32[]{:S(2)}) collective-permute-start(bf16[512,128]{1,0:T(8,128)(2,1)S(1)} %convolution_convert_fusion.3), channel_id=1, source_target_pairs={{0,8},{4,12},{8,16},{12,20},{16,24},{20,28},{1,9},{5,13},{9,17},{1... | collective-permute-start | bytes 393224 | tf_op jit(solution)/shard_map/ppermute | solution.py:13
  84.6 13.5 %collective-permute-start.3 = (bf16[512,128]{1,0:T(8,128)(2,1)S(1)}, bf16[512,128]{1,0:T(8,128)(2,1)}, u32[]{:S(2)}, u32[]{:S(2)}) collective-permute-start(bf16[512,128]{1,0:T(8,128)(2,1)S(1)} %convolution_convert_fusion.3), channel_id=1, source_target_pairs={{0,4},{4,8},{8,12},{12,16},{16,20},{20,24},{24,28},{1,5},{5,9},{9,... | collective-permute-start | bytes 393224 | tf_op jit(solution)/shard_map/ppermute | solution.py:13
  89.6 14.5 %collective-permute-start = (bf16[512,128]{1,0:T(8,128)(2,1)S(1)}, bf16[512,128]{1,0:T(8,128)(2,1)S(1)}, u32[]{:S(2)}, u32[]{:S(2)}) collective-permute-start(bf16[512,128]{1,0:T(8,128)(2,1)S(1)} %convolution_convert_fusion.4), channel_id=1, source_target_pairs={{0,8},{4,12},{8,16},{12,20},{16,24},{20,28},{1,9},{5,13},{9,17},{1... | collective-permute-start | bytes 393224 | tf_op jit(solution)/shard_map/ppermute | solution.py:13
  92.4 11.8 %collective-permute-start.1 = (bf16[512,128]{1,0:T(8,128)(2,1)S(1)}, bf16[512,128]{1,0:T(8,128)(2,1)S(1)}, u32[]{:S(2)}, u32[]{:S(2)}) collective-permute-start(bf16[512,128]{1,0:T(8,128)(2,1)S(1)} %convolution_convert_fusion.4), channel_id=1, source_target_pairs={{0,4},{4,8},{8,12},{12,16},{16,20},{20,24},{24,28},{1,5},{5,9},{9,... | collective-permute-start | bytes 393224 | tf_op jit(solution)/shard_map/ppermute | solution.py:13
  147.1 144.2 %copy-start.4 = (f32[2048]{0:T(1024)S(1)}, f32[2048]{0:T(1024)}, u32[]{:S(2)}) copy-start(f32[2048]{0:T(1024)} %param.16) | copy-start | bytes 24580
  147.1 144.1 %all-gather.13.cloned.1.call-start = ((), (), s32[]{:S(2)}) async-start(), calls=%async_computation.5 | async-start | bytes 6488064 | tf_op jit(solution)/shard_map/all_gather | solution.py:88
  147.7 236.1 %all-gather.15.cloned.1.call-start = ((), (), s32[]{:S(2)}) async-start(), calls=%async_computation.6 | async-start | bytes 6488064 | tf_op jit(solution)/shard_map/all_gather | solution.py:89
  148.3 328.9 %all-gather.17.cloned.1.call-start = ((), (), s32[]{:S(2)}) async-start(), calls=%async_computation.7 | async-start | bytes 6488064 | tf_op jit(solution)/shard_map/all_gather | solution.py:93
  149.1 371.1 %reduce-scatter.2.cloned.1.call-start = ((), (), s32[]{:S(2)}) async-start(), calls=%async_computation.8 | async-start | bytes 2621440 | tf_op jit(solution)/shard_map/reduce_scatter | solution.py:95
  291.3 185.9 %copy-start.1 = (bf16[512,2048]{1,0:T(8,128)(2,1)S(1)}, bf16[512,2048]{1,0:T(8,128)(2,1)}, u32[]{:S(2)}) copy-start(bf16[512,2048]{1,0:T(8,128)(2,1)} %get-tuple-element.6) | copy-start | bytes 6291460
Sparse Core Ops, SparseCore 0:
  8.9 25.2 all-gather.6
  36.3 52.5 all-gather.8
  91.0 51.7 all-gather.10
  147.3 49.5 all-reduce.1
  198.9 92.3 all-gather.12
  293.3 90.4 all-gather.14
  385.9 91.2 all-gather.16
  490.8 29.3 reduce-scatter.1
where the time goes:
time: 529 us
  waiting for transfers between devices  383 us (72%)
  blocking collectives  68.5 us (13%)
  matrix products  40.5 us (8%)
  between operations  13.7 us (3%)
  other arithmetic  12.2 us (2%)
  starting transfers between devices  11.5 us (2%)
    all_gather x1, waiting for transfers between devices, per_device(): down_full = lax.all_gather(w_down, 'seq', axis=1, tiled=True)  93.4 us
    all_gather x1, waiting for transfers between devices, per_device(): gate_full = lax.all_gather(w_gate, 'seq', axis=0, tiled=True)  90.5 us
    all_gather x1, waiting for transfers between devices, per_device(): up_full = lax.all_gather(w_up, 'seq', axis=0, tiled=True)  84.1 us
    psum x1, waiting for transfers between devices, per_device(): lax.psum(head_terms.astype(jnp.bfloat16), 'tensor').astype(jnp.float32)  47.5 us
    all_gather x1, blocking collectives, per_device(): lax.all_gather(w_value, 'seq', axis=0, tiled=True)  35.2 us
    all_gather x1, waiting for transfers between devices, per_device(): out_full = lax.all_gather(w_out, 'seq', axis=1, tiled=True)  33.7 us
    all_gather x1, blocking collectives, per_device(): lax.all_gather(w_key, 'seq', axis=0, tiled=True)  33.4 us
    dot_general x6, matrix products, product(): return jnp.dot(left, right, preferred_element_type=jnp.float32)  32.3 us
  transfers between devices with their start and end apart: 12, of which 6 were waited for; matrix products, arithmetic and copies ran while one was open for 6% of the time, Pallas kernels for 0%

commit v1 on v0

--- a/solution.py
+++ b/solution.py
@@ -90,7 +90,12 @@
     gate = product(stream_normed, gate_full)
     upward = product(stream_normed, up_full)
     hidden = (jax.nn.silu(gate) * upward).astype(jnp.bfloat16)
-    down_full = lax.all_gather(w_down, "seq", axis=1, tiled=True)
+    ring = [w_down]
+    for hop in range(7):
+        ring.append(lax.ppermute(ring[-1], "seq", [(dev, (dev + 1) % 8) for dev in range(8)]))
+    down_full = jnp.roll(
+        jnp.concatenate(ring[::-1], axis=1), (lax.axis_index("seq") + 1) * ring[0].shape[1], axis=1
+    )
     unit_terms = product(hidden, down_full)
     mlp_share = lax.psum_scatter(
         unit_terms.astype(jnp.bfloat16), "tensor", scatter_dimension=1, tiled=True

time: 529 us -> 485 us (0.917)
  waiting for transfers between devices: 383 us -> 314 us
  local copies, waits for them, and re-layouts: 0.02 us -> 23.6 us
    ppermute x0 -> x7, waiting for transfers between devices: none -> 177 us  [per_device(): lax.ppermute(ring[-1], 'seq', [(dev, (dev + 1) % 8) for dev in range(8)])]
    all_gather x1 -> x0, waiting for transfers between devices: 93.4 us -> none  [per_device(): down_full = lax.all_gather(w_down, 'seq', axis=1, tiled=True)]
    all_gather x1, waiting for transfers between devices: 90.5 us -> 0.01 us  [per_device(): gate_full = lax.all_gather(w_gate, 'seq', axis=0, tiled=True)]
    psum x1, waiting for transfers between devices: 47.5 us -> 0.01 us  [per_device(): lax.psum(head_terms.astype(jnp.bfloat16), 'tensor').astype(jnp.float32)]
    unnamed x10 -> x43, local copies, waits for them, and re-layouts: 0.02 us -> 22.7 us
    all_gather x1, waiting for transfers between devices: 84.1 us -> 70.8 us  [per_device(): up_full = lax.all_gather(w_up, 'seq', axis=0, tiled=True)]
  transfers between devices with their start and end apart: 12 -> 18, of which waited for: 6 -> 10; matrix products, arithmetic and copies ran while one was open for 6% -> 11% of each run, Pallas kernels for 0% -> 0%
where the time goes in v1:
time: 485 us
  waiting for transfers between devices  314 us (65%)
  blocking collectives  68.5 us (14%)
  matrix products  39.7 us (8%)
  local copies, waits for them, and re-layouts  23.6 us (5%)
  between operations  13.7 us (3%)
  starting transfers between devices  12.7 us (3%)
  other arithmetic  12.3 us (3%)
    ppermute x7, waiting for transfers between devices, per_device(): lax.ppermute(ring[-1], 'seq', [(dev, (dev + 1) % 8) for dev in range(8)])  177 us
    all_gather x1, waiting for transfers between devices, per_device(): up_full = lax.all_gather(w_up, 'seq', axis=0, tiled=True)  70.8 us
    all_gather x1, blocking collectives, per_device(): lax.all_gather(w_value, 'seq', axis=0, tiled=True)  35.2 us
    all_gather x1, waiting for transfers between devices, per_device(): out_full = lax.all_gather(w_out, 'seq', axis=1, tiled=True)  33.7 us
    all_gather x1, blocking collectives, per_device(): lax.all_gather(w_key, 'seq', axis=0, tiled=True)  33.4 us
    dot_general x6, matrix products, product(): return jnp.dot(left, right, preferred_element_type=jnp.float32)  31.6 us
    reduce_scatter x1, waiting for transfers between devices, per_device(): lax.psum_scatter(unit_terms.astype(jnp.bfloat16), 'tensor', scatter_dimen...  29.5 us
    unnamed x43, local copies, waits for them, and re-layouts  22.7 us
  transfers between devices with their start and end apart: 18, of which 10 were waited for; matrix products, arithmetic and copies ran while one was open for 11% of the time, Pallas kernels for 0%

profile of v1, /device:TPU:0, one launch (start us, length us, event | category | flops | bytes accessed | tf_op | source)
XLA Modules:
  0.0 484.6 jit_solution(8302049509703774637)
XLA Ops:
  6.5 0.7 all-gather.6.cloned.1.call-update
  7.3 0.0 all-gather.8.cloned.1.call-start
  7.3 0.7 all-gather.8.cloned.1.call-update
  8.0 0.0 all-gather.10.cloned.1.call-start
  8.1 0.7 all-gather.10.cloned.1.call-update
  8.7 0.0 all-reduce.2.cloned.1.call-start
  8.8 33.4 %all_gather.23 = bf16[2048,128]{1,0:T(8,128)(2,1)S(1)} all-gather(bf16[256,128]{1,0:T(8,128)(2,1)} %param.13), channel_id=1, replica_groups=mesh['seq'=8,'tensor'=4] {'seq'}, dimensions={0}, use_global_device_ids=true | all-gather | bytes 589824 | tf_op jit(solution)/shard_map/all_gather | solution.py:61
  42.2 35.2 %all_gather.22 = bf16[2048,128]{1,0:T(8,128)(2,1)} all-gather(bf16[256,128]{1,0:T(8,128)(2,1)} %param.14), channel_id=1, replica_groups=mesh['seq'=8,'tensor'=4] {'seq'}, dimensions={0}, use_global_device_ids=true | all-gather | bytes 589824 | tf_op jit(solution)/shard_map/all_gather | solution.py:62
  77.3 1.3 fusion.16
  78.6 0.0 all-gather.6.cloned.1.call-done
  78.7 2.2 fusion.9
  80.9 2.4 convolution_convert_fusion.2
  83.3 1.3 collective-permute-start.2
  84.6 4.3 collective-permute-start.3
  88.9 0.8 convolution_convert_fusion.3
  89.6 2.7 collective-permute-start
  92.4 2.7 collective-permute-start.1
  95.1 0.0 all-gather.8.cloned.1.call-done
  95.1 3.0 convolution_convert_fusion.1
  98.1 3.3 fusion.1
  101.4 2.8 fusion
  104.2 4.8 fusion.21
  109.0 33.7 %all-gather.10.cloned.1.call-done = bf16[512,2048]{1,0:T(8,128)(2,1)} async-done(((bf16[512,256]{1,0:T(8,128)(2,1)}), bf16[512,2048]{1,0:T(8,128)(2,1)}) %all-gather.10.cloned.1.call-update) | async-done | bytes 2097168 | tf_op jit(solution)/shard_map/all_gather | solution.py:79
  142.7 4.4 convolution_convert_fusion
  147.1 0.0 all-reduce.2.cloned.1.call-update
  147.2 0.0 all-gather.12.cloned.1.call-start
  147.2 0.5 all-gather.12.cloned.1.call-update
  147.7 0.0 all-gather.14.cloned.1.call-start
  147.8 0.5 all-gather.14.cloned.1.call-update
  148.3 0.0 reduce-scatter.2.cloned.1.call-start
  148.4 1.5 collective-permute-start.4
  149.9 18.3 %collective-permute-done.4 = bf16[1408,256]{1,0:T(8,128)(2,1)S(1)} collective-permute-done((bf16[1408,256]{1,0:T(8,128)(2,1)S(1)}, bf16[1408,256]{1,0:T(8,128)(2,1)S(1)}, u32[]{:S(2)}, u32[]{:S(2)}) %collective-permute-start.4) | collective-permute-done | bytes 720928 | tf_op jit(solution)/shard_map/ppermute | solution.py:95
  168.2 18.9 %collective-permute-done.5 = bf16[1408,256]{1,0:T(8,128)(2,1)S(1)} collective-permute-done((bf16[1408,256]{1,0:T(8,128)(2,1)S(1)}, bf16[1408,256]{1,0:T(8,128)(2,1)S(1)}, u32[]{:S(2)}, u32[]{:S(2)}) %collective-permute-start.5) | collective-permute-done | bytes 720928 | tf_op jit(solution)/shard_map/ppermute | solution.py:95
  187.0 0.9 copy-done.3
  187.9 18.0 %collective-permute-done.6 = bf16[1408,256]{1,0:T(8,128)(2,1)S(1)} collective-permute-done((bf16[1408,256]{1,0:T(8,128)(2,1)S(1)}, bf16[1408,256]{1,0:T(8,128)(2,1)S(1)}, u32[]{:S(2)}, u32[]{:S(2)}) %collective-permute-start.6) | collective-permute-done | bytes 720928 | tf_op jit(solution)/shard_map/ppermute | solution.py:95
  205.9 0.9 copy-done.5
  206.8 35.0 %collective-permute-done.7 = bf16[1408,256]{1,0:T(8,128)(2,1)S(1)} collective-permute-done((bf16[1408,256]{1,0:T(8,128)(2,1)S(1)}, bf16[1408,256]{1,0:T(8,128)(2,1)S(1)}, u32[]{:S(2)}, u32[]{:S(2)}) %collective-permute-start.7) | collective-permute-done | bytes 720928 | tf_op jit(solution)/shard_map/ppermute | solution.py:95
  241.8 0.9 copy-done.7
  242.7 20.0 %collective-permute-done.8 = bf16[1408,256]{1,0:T(8,128)(2,1)S(1)} collective-permute-done((bf16[1408,256]{1,0:T(8,128)(2,1)S(1)}, bf16[1408,256]{1,0:T(8,128)(2,1)S(1)}, u32[]{:S(2)}, u32[]{:S(2)}) %collective-permute-start.8) | collective-permute-done | bytes 720928 | tf_op jit(solution)/shard_map/ppermute | solution.py:95
  262.7 0.9 copy-done.9
  263.6 35.4 %collective-permute-done.9 = bf16[1408,256]{1,0:T(8,128)(2,1)} collective-permute-done((bf16[1408,256]{1,0:T(8,128)(2,1)S(1)}, bf16[1408,256]{1,0:T(8,128)(2,1)}, u32[]{:S(2)}, u32[]{:S(2)}) %collective-permute-start.9) | collective-permute-done | bytes 720928 | tf_op jit(solution)/shard_map/ppermute | solution.py:95
  299.0 4.1 fusion.6
  303.1 31.2 %collective-permute-done.10 = bf16[1408,256]{1,0:T(8,128)(2,1)} collective-permute-done((bf16[1408,256]{1,0:T(8,128)(2,1)}, bf16[1408,256]{1,0:T(8,128)(2,1)}, u32[]{:S(2)}, u32[]{:S(2)}) %collective-permute-start.10) | collective-permute-done | bytes 720928 | tf_op jit(solution)/shard_map/ppermute | solution.py:95
  334.3 2.1 constant_dynamic-update-slice_fusion.15
  336.4 2.1 constant_dynamic-update-slice_fusion.14
  338.5 1.0 constant_dynamic-update-slice_fusion.13
  339.5 1.0 constant_dynamic-update-slice_fusion.12
  340.5 1.0 constant_dynamic-update-slice_fusion.11
  341.5 1.0 constant_dynamic-update-slice_fusion.10
  342.4 1.0 constant_dynamic-update-slice_fusion.9
  343.4 1.0 constant_dynamic-update-slice_fusion.8
  344.4 2.1 constant_dynamic-update-slice_fusion.7
  346.5 2.1 constant_dynamic-update-slice_fusion.6
  348.6 1.0 constant_dynamic-update-slice_fusion.5
  349.6 1.0 constant_dynamic-update-slice_fusion.4
  350.6 1.0 constant_dynamic-update-slice_fusion.3
  351.6 1.0 constant_dynamic-update-slice_fusion.2
  352.5 1.0 constant_dynamic-update-slice_fusion.1
  353.5 0.9 constant_dynamic-update-slice_fusion
  354.4 7.7 %fusion.26 = f32[512,1408]{1,0:T(8,128)} fusion(bf16[2048,1408]{1,0:T(8,128)(2,1)} %all-gather.12.cloned.1.call-done, bf16[512,2048]{1,0:T(8,128)(2,1)S(1)} %copy-done.1, f32[2048]{0:T(1024)S(1)} %copy-done.13, f32[512]{0:T(512)S(1)} %add_rsqrt_fusion), kind=kOutput, calls=%fused_computation.35 | convolution fusion | flops 2956984320 | bytes 10758144 | tf_op jit(solution)/shard_map/dot_general | solution.py:23
  362.2 70.8 %all-gather.14.cloned.1.call-done = bf16[2048,1408]{1,0:T(8,128)(2,1)} async-done(((bf16[256,1408]{1,0:T(8,128)(2,1)}), bf16[2048,1408]{1,0:T(8,128)(2,1)}) %all-gather.14.cloned.1.call-update) | async-done | bytes 5767184 | tf_op jit(solution)/shard_map/all_gather | solution.py:89
  433.0 13.3 %fusion.18 = bf16[512,2048]{1,0:T(8,128)(2,1)} fusion(bf16[1408,4096]{1,0:T(8,128)(2,1)} %constant_dynamic-update-slice_fusion, s32[]{:T(128)S(6)} %select_n.23, bf16[2048,1408]{1,0:T(8,128)(2,1)} %all-gather.14.cloned.1.call-done, f32[512,1408]{1,0:T(8,128)} %fusion.26, bf16[512,2048]{1,0:T(8,128)(2,1)S(1)} %copy-done.1, f32[2048]{0:T(1024)S(1)} %copy-done.13, ...), kind=kOutput, calls=%fused_computation.28 | convolution fusion | flops 5915148288 | bytes 18622468 | tf_op jit(solution)/shard_map/dot_general | solution.py:23
  446.3 29.5 %reduce-scatter.2.cloned.1.call-done = bf16[512,512]{1,0:T(8,128)(2,1)} async-done(((bf16[512,2048]{1,0:T(8,128)(2,1)}), bf16[512,512]{1,0:T(8,128)(2,1)}) %reduce-scatter.2.cloned.1.call-update) | async-done | bytes 524304 | tf_op jit(solution)/shard_map/reduce_scatter | solution.py:100
  475.8 2.0 add_convert_fusion
  (42 shorter events, 0.1 us)
Async XLA Ops:
  6.5 74.4 %copy-start.12 = (f32[2048]{0:T(1024)S(1)}, f32[2048]{0:T(1024)}, u32[]{:S(2)}) copy-start(f32[2048]{0:T(1024)} %param.11) | copy-start | bytes 24580
  6.5 72.1 %all-gather.6.cloned.1.call-start = ((), (), s32[]{:S(2)}) async-start(), calls=%async_computation.1 | async-start | bytes 2621440 | tf_op jit(solution)/shard_map/all_gather | solution.py:57
  7.3 87.8 %all-gather.8.cloned.1.call-start = ((), (), s32[]{:S(2)}) async-start(), calls=%async_computation.2 | async-start | bytes 2359296 | tf_op jit(solution)/shard_map/all_gather | solution.py:59
  8.0 134.7 %all-gather.10.cloned.1.call-start = ((), (), s32[]{:S(2)}) async-start(), calls=%async_computation.3 | async-start | bytes 2359296 | tf_op jit(solution)/shard_map/all_gather | solution.py:79
  8.7 290.2 %all-reduce.2.cloned.1.call-start = ((), (), s32[]{:S(2)}) async-start(), calls=%async_computation.4 | async-start | bytes 4194304 | tf_op jit(solution)/shard_map/psum | solution.py:82
  78.6 10.2 %copy-start = (bf16[512,2048]{1,0:T(8,128)(2,1)S(1)}, bf16[512,2048]{1,0:T(8,128)(2,1)}, u32[]{:S(2)}) copy-start(bf16[512,2048]{1,0:T(8,128)(2,1)} %all-gather.6.cloned.1.call-done) | copy-start | bytes 6291460
  78.7 10.2 %copy-start.11 = (bf16[2048,128]{1,0:T(8,128)(2,1)S(1)}, bf16[2048,128]{1,0:T(8,128)(2,1)}, u32[]{:S(2)}) copy-start(bf16[2048,128]{1,0:T(8,128)(2,1)} %all_gather.22) | copy-start | bytes 1572868
  83.3 14.8 %collective-permute-start.2 = (bf16[512,128]{1,0:T(8,128)(2,1)S(1)}, bf16[512,128]{1,0:T(8,128)(2,1)S(1)}, u32[]{:S(2)}, u32[]{:S(2)}) collective-permute-start(bf16[512,128]{1,0:T(8,128)(2,1)S(1)} %convolution_convert_fusion.2), channel_id=1, source_target_pairs={{0,8},{4,12},{8,16},{12,20},{16,24},{20,28},{1,9},{5,13},{9,17},{1... | collective-permute-start | bytes 393224 | tf_op jit(solution)/shard_map/ppermute | solution.py:13
  84.6 13.5 %collective-permute-start.3 = (bf16[512,128]{1,0:T(8,128)(2,1)S(1)}, bf16[512,128]{1,0:T(8,128)(2,1)}, u32[]{:S(2)}, u32[]{:S(2)}) collective-permute-start(bf16[512,128]{1,0:T(8,128)(2,1)S(1)} %convolution_convert_fusion.2), channel_id=1, source_target_pairs={{0,4},{4,8},{8,12},{12,16},{16,20},{20,24},{24,28},{1,5},{5,9},{9,... | collective-permute-start | bytes 393224 | tf_op jit(solution)/shard_map/ppermute | solution.py:13
  89.6 14.5 %collective-permute-start = (bf16[512,128]{1,0:T(8,128)(2,1)S(1)}, bf16[512,128]{1,0:T(8,128)(2,1)S(1)}, u32[]{:S(2)}, u32[]{:S(2)}) collective-permute-start(bf16[512,128]{1,0:T(8,128)(2,1)S(1)} %convolution_convert_fusion.3), channel_id=1, source_target_pairs={{0,8},{4,12},{8,16},{12,20},{16,24},{20,28},{1,9},{5,13},{9,17},{1... | collective-permute-start | bytes 393224 | tf_op jit(solution)/shard_map/ppermute | solution.py:13
  92.4 11.8 %collective-permute-start.1 = (bf16[512,128]{1,0:T(8,128)(2,1)S(1)}, bf16[512,128]{1,0:T(8,128)(2,1)S(1)}, u32[]{:S(2)}, u32[]{:S(2)}) collective-permute-start(bf16[512,128]{1,0:T(8,128)(2,1)S(1)} %convolution_convert_fusion.3), channel_id=1, source_target_pairs={{0,4},{4,8},{8,12},{12,16},{16,20},{20,24},{24,28},{1,5},{5,9},{9,... | collective-permute-start | bytes 393224 | tf_op jit(solution)/shard_map/ppermute | solution.py:13
  142.7 5.6 %copy-start.2 = (bf16[1408,256]{1,0:T(8,128)(2,1)S(1)}, bf16[1408,256]{1,0:T(8,128)(2,1)}, u32[]{:S(2)}) copy-start(bf16[1408,256]{1,0:T(8,128)(2,1)} %param.19) | copy-start | bytes 2162692
  147.2 207.2 %all-gather.12.cloned.1.call-start = ((), (), s32[]{:S(2)}) async-start(), calls=%async_computation.5 | async-start | bytes 6488064 | tf_op jit(solution)/shard_map/all_gather | solution.py:88
  147.7 285.2 %all-gather.14.cloned.1.call-start = ((), (), s32[]{:S(2)}) async-start(), calls=%async_computation.6 | async-start | bytes 6488064 | tf_op jit(solution)/shard_map/all_gather | solution.py:89
  148.3 327.5 %reduce-scatter.2.cloned.1.call-start = ((), (), s32[]{:S(2)}) async-start(), calls=%async_computation.7 | async-start | bytes 2621440 | tf_op jit(solution)/shard_map/reduce_scatter | solution.py:100
  148.4 19.8 %collective-permute-start.4 = (bf16[1408,256]{1,0:T(8,128)(2,1)S(1)}, bf16[1408,256]{1,0:T(8,128)(2,1)S(1)}, u32[]{:S(2)}, u32[]{:S(2)}) collective-permute-start(bf16[1408,256]{1,0:T(8,128)(2,1)S(1)} %copy-done.2), channel_id=1, source_target_pairs={{0,4},{4,8},{8,12},{12,16},{16,20},{20,24},{24,28},{28,0},{1,5},{5... | collective-permute-start | bytes 2162696 | tf_op jit(solution)/shard_map/ppermute | solution.py:95
  168.2 18.9 %collective-permute-start.5 = (bf16[1408,256]{1,0:T(8,128)(2,1)S(1)}, bf16[1408,256]{1,0:T(8,128)(2,1)S(1)}, u32[]{:S(2)}, u32[]{:S(2)}) collective-permute-start(bf16[1408,256]{1,0:T(8,128)(2,1)S(1)} %collective-permute-done.4), channel_id=1, source_target_pairs={{0,4},{4,8},{8,12},{12,16},{16,20},{20,24},{24,28},{28,0},{1,5},{5... | collective-permute-start | bytes 2162696 | tf_op jit(solution)/shard_map/ppermute | solution.py:95
  187.0 0.9 copy-start.3
  187.9 18.0 %collective-permute-start.6 = (bf16[1408,256]{1,0:T(8,128)(2,1)S(1)}, bf16[1408,256]{1,0:T(8,128)(2,1)S(1)}, u32[]{:S(2)}, u32[]{:S(2)}) collective-permute-start(bf16[1408,256]{1,0:T(8,128)(2,1)S(1)} %collective-permute-done.5), channel_id=1, source_target_pairs={{0,4},{4,8},{8,12},{12,16},{16,20},{20,24},{24,28},{28,0},{1,5},{5... | collective-permute-start | bytes 2162696 | tf_op jit(solution)/shard_map/ppermute | solution.py:95
  205.9 0.9 copy-start.5
  206.8 35.0 %collective-permute-start.7 = (bf16[1408,256]{1,0:T(8,128)(2,1)S(1)}, bf16[1408,256]{1,0:T(8,128)(2,1)S(1)}, u32[]{:S(2)}, u32[]{:S(2)}) collective-permute-start(bf16[1408,256]{1,0:T(8,128)(2,1)S(1)} %collective-permute-done.6), channel_id=1, source_target_pairs={{0,4},{4,8},{8,12},{12,16},{16,20},{20,24},{24,28},{28,0},{1,5},{5... | collective-permute-start | bytes 2162696 | tf_op jit(solution)/shard_map/ppermute | solution.py:95
  241.8 0.9 copy-start.7
  242.7 20.0 %collective-permute-start.8 = (bf16[1408,256]{1,0:T(8,128)(2,1)S(1)}, bf16[1408,256]{1,0:T(8,128)(2,1)S(1)}, u32[]{:S(2)}, u32[]{:S(2)}) collective-permute-start(bf16[1408,256]{1,0:T(8,128)(2,1)S(1)} %collective-permute-done.7), channel_id=1, source_target_pairs={{0,4},{4,8},{8,12},{12,16},{16,20},{20,24},{24,28},{28,0},{1,5},{5... | collective-permute-start | bytes 2162696 | tf_op jit(solution)/shard_map/ppermute | solution.py:95
  262.7 0.9 copy-start.9
  263.6 35.4 %collective-permute-start.9 = (bf16[1408,256]{1,0:T(8,128)(2,1)S(1)}, bf16[1408,256]{1,0:T(8,128)(2,1)}, u32[]{:S(2)}, u32[]{:S(2)}) collective-permute-start(bf16[1408,256]{1,0:T(8,128)(2,1)S(1)} %collective-permute-done.8), channel_id=1, source_target_pairs={{0,4},{4,8},{8,12},{12,16},{16,20},{20,24},{24,28},{28,0},{1,5},{5... | collective-permute-start | bytes 2162696 | tf_op jit(solution)/shard_map/ppermute | solution.py:95
  299.0 35.3 %collective-permute-start.10 = (bf16[1408,256]{1,0:T(8,128)(2,1)}, bf16[1408,256]{1,0:T(8,128)(2,1)}, u32[]{:S(2)}, u32[]{:S(2)}) collective-permute-start(bf16[1408,256]{1,0:T(8,128)(2,1)} %collective-permute-done.9), channel_id=1, source_target_pairs={{0,4},{4,8},{8,12},{12,16},{16,20},{20,24},{24,28},{28,0},{1,5},{5... | collective-permute-start | bytes 2162696 | tf_op jit(solution)/shard_map/ppermute | solution.py:95
  299.0 39.5 %copy-start.10 = (bf16[1408,256]{1,0:T(8,128)(2,1)S(1)}, bf16[1408,256]{1,0:T(8,128)(2,1)}, u32[]{:S(2)}) copy-start(bf16[1408,256]{1,0:T(8,128)(2,1)} %copy-done.9) | copy-start | bytes 2162692
  299.0 40.5 %copy-start.8 = (bf16[1408,256]{1,0:T(8,128)(2,1)S(1)}, bf16[1408,256]{1,0:T(8,128)(2,1)}, u32[]{:S(2)}) copy-start(bf16[1408,256]{1,0:T(8,128)(2,1)} %copy-done.7) | copy-start | bytes 2162692
  303.1 37.4 %copy-start.6 = (bf16[1408,256]{1,0:T(8,128)(2,1)S(1)}, bf16[1408,256]{1,0:T(8,128)(2,1)}, u32[]{:S(2)}) copy-start(bf16[1408,256]{1,0:T(8,128)(2,1)} %copy-done.5) | copy-start | bytes 2162692
  303.1 38.4 %copy-start.4 = (bf16[1408,256]{1,0:T(8,128)(2,1)S(1)}, bf16[1408,256]{1,0:T(8,128)(2,1)}, u32[]{:S(2)}) copy-start(bf16[1408,256]{1,0:T(8,128)(2,1)} %copy-done.3) | copy-start | bytes 2162692
  348.6 5.8 %copy-start.1 = (bf16[512,2048]{1,0:T(8,128)(2,1)S(1)}, bf16[512,2048]{1,0:T(8,128)(2,1)}, u32[]{:S(2)}) copy-start(bf16[512,2048]{1,0:T(8,128)(2,1)} %get-tuple-element.6) | copy-start | bytes 6291460
  348.6 5.8 %copy-start.13 = (f32[2048]{0:T(1024)S(1)}, f32[2048]{0:T(1024)}, u32[]{:S(2)}) copy-start(f32[2048]{0:T(1024)} %param.16) | copy-start | bytes 24580
Sparse Core Ops, SparseCore 0:
  8.9 25.2 all-gather.5
  36.3 52.5 all-gather.7
  91.0 51.7 all-gather.9
  147.3 49.5 all-reduce.1
  198.9 135.5 all-gather.11
  336.6 96.3 all-gather.13
  446.4 29.3 reduce-scatter.1
